TPU v7x, 32 devices: a whole 2x2x4 slice. The times are simulated.
32 devices in a mesh: owner: 4 (over y, core), rows: 8 (over z, x).
Axes of the slice: x: 2, y: 2, z: 4, core: 2. Of those that a mesh axis runs over, the one named last changes fastest.
Arguments:
- train_gate: float32 [128, 2048, 768], P('owner', 'rows'), may hold values from -0.125 to 0.125
- train_up: float32 [128, 2048, 768], P('owner', 'rows'), may hold values from -0.125 to 0.125
- router_weight: float32 [2048, 128], P('rows', 'owner'), may hold values from -0.125 to 0.125
- router_gain: float32 [2048], P('rows'), may hold values from 0.25 to 1.75
Outputs:
- ready_gate: bfloat16 [128, 768, 2048], P(('owner', 'rows'))
- ready_up: bfloat16 [128, 768, 2048], P(('owner', 'rows'))
- serve_router: bfloat16 [2048, 128], replicated
All inputs are finite; a program needn't handle non-finite values.
Results may differ from a plain program's by a relative error of at most 0.001.
Values may be sent and summed in bfloat16 or wider, within the bound.
A program may use at most 192 MiB of HBM per device.

v0:
```python
import jax
import jax.numpy as jnp
from jax import lax
from jax.sharding import PartitionSpec as P


def on_device(train_gate, train_up, router_weight, router_gain):
    narrow_gate, narrow_up = (train_gate.astype(jnp.bfloat16), train_up.astype(jnp.bfloat16))
    ready_gate, ready_up = (
        lax.all_to_all(narrow_gate, "rows", split_axis=0, concat_axis=1, tiled=True),
        lax.all_to_all(narrow_up, "rows", split_axis=0, concat_axis=1, tiled=True),
    )
    ready_gate = jnp.transpose(ready_gate, (0, 2, 1))
    ready_up = jnp.transpose(ready_up, (0, 2, 1))
    part_router = (router_weight * router_gain[:, None]).astype(jnp.bfloat16)
    row_router = lax.all_gather(part_router, "rows", axis=0, tiled=True)
    serve_router = lax.all_gather(row_router, "owner", axis=1, tiled=True)
    return (ready_gate, ready_up, serve_router)


def solution(mesh):
    placed = (P("owner", "rows", None), P("owner", "rows", None), P("rows", "owner"), P("rows"))
    return jax.shard_map(
        on_device,
        mesh=mesh,
        in_specs=placed,
        out_specs=(P(("owner", "rows"), None, None), P(("owner", "rows"), None, None), P()),
        check_vma=False,
    )
```

profile of v0, /device:TPU:0, one launch (start us, length us, event | category | flops | bytes accessed | tf_op | source)
XLA Modules:
  0.0 672.7 jit_solution(13268045616997217038)
XLA Ops:
  0.6 13.2 %convert_element_type.9 = bf16[32,256,768]{2,1,0:T(8,128)(2,1)} convert(f32[32,256,768]{2,1,0:T(8,128)} %param.4) | non-fusion elementwise | flops 6291456 | bytes 37748736 | tf_op jit(solution)/shard_map/convert_element_type | solution.py:8
  13.8 7.3 %all-to-all-start = ((bf16[32,256,768]{2,1,0:T(8,128)(2,1)}), bf16[32,256,768]{2,1,0:T(8,128)(2,1)}, u32[]{:S(2)}, u32[]{:S(2)}) async-start(bf16[32,256,768]{2,1,0:T(8,128)(2,1)} %convert_element_type.9), calls=%async_computation | async-start | bytes 25165824 | tf_op jit(solution)/shard_map/all_to_all | solution.py:10
  21.1 13.4 %convert_element_type.10 = bf16[32,256,768]{2,1,0:T(8,128)(2,1)} convert(f32[32,256,768]{2,1,0:T(8,128)} %param.5) | non-fusion elementwise | flops 6291456 | bytes 37748736 | tf_op jit(solution)/shard_map/convert_element_type | solution.py:8
  34.5 0.0 copy-start
  34.5 0.0 copy-start.1
  34.5 259.7 %all-to-all-done = bf16[32,256,768]{2,1,0:T(8,128)(2,1)} async-done(((bf16[32,256,768]{2,1,0:T(8,128)(2,1)}), bf16[32,256,768]{2,1,0:T(8,128)(2,1)}, u32[]{:S(2)}, u32[]{:S(2)}) %all-to-all-start) | async-done | bytes 12582944 | tf_op jit(solution)/shard_map/all_to_all | solution.py:10
  294.2 5.3 all-to-all-start.1
  299.5 0.0 copy-done
  299.5 0.0 copy-done.1
  299.5 292.2 %all_gather.6 = bf16[2048,32]{0,1:T(8,128)(2,1)S(1)} all-gather(bf16[256,32]{0,1:T(8,128)(2,1)S(1)} %multiply_convert_fusion), channel_id=1, replica_groups=mesh['owner'=4,'rows'=8] {'rows'}, dimensions={0}, use_global_device_ids=true | all-gather | bytes 147456 | tf_op jit(solution)/shard_map/all_gather | solution.py:16
  591.8 7.2 %all_gather.7 = bf16[2048,128]{0,1:T(8,128)(2,1)S(1)} all-gather(bf16[2048,32]{0,1:T(8,128)(2,1)S(1)} %all_gather.6), channel_id=1, replica_groups=mesh['owner'=4,'rows'=8] {'owner'}, dimensions={1}, use_global_device_ids=true | all-gather | bytes 655360 | tf_op jit(solution)/shard_map/all_gather | solution.py:17
  598.9 1.0 copy.12
  599.9 16.9 %copy.10 = bf16[8,4,256,768]{2,0,3,1:T(8,128)(2,1)} copy(bf16[8,4,256,768]{3,2,1,0:T(8,128)(2,1)} %bitcast) | data formatting | bytes 25165824 | tf_op jit(solution)/shard_map/all_to_all | solution.py:10
  616.8 19.5 %all_to_all.29 = bf16[4,2048,768]{1,2,0:T(8,128)(2,1)} reshape(bf16[4,8,256,768]{2,1,3,0:T(8,128)(2,1)} %bitcast.14) | data formatting | bytes 25165824 | tf_op jit(solution)/shard_map/all_to_all | solution.py:10
  636.3 0.0 all-to-all-done.1
  636.3 16.9 %copy.11 = bf16[8,4,256,768]{2,0,3,1:T(8,128)(2,1)} copy(bf16[8,4,256,768]{3,2,1,0:T(8,128)(2,1)} %bitcast.3) | data formatting | bytes 25165824 | tf_op jit(solution)/shard_map/all_to_all | solution.py:11
  653.2 19.5 %all_to_all.33 = bf16[4,2048,768]{1,2,0:T(8,128)(2,1)} reshape(bf16[4,8,256,768]{2,1,3,0:T(8,128)(2,1)} %bitcast.15) | data formatting | bytes 25165824 | tf_op jit(solution)/shard_map/all_to_all | solution.py:11
  (1 shorter events, 0.0 us)
Async XLA Ops:
  13.8 280.3 %all-to-all-start = ((bf16[32,256,768]{2,1,0:T(8,128)(2,1)}), bf16[32,256,768]{2,1,0:T(8,128)(2,1)}, u32[]{:S(2)}, u32[]{:S(2)}) async-start(bf16[32,256,768]{2,1,0:T(8,128)(2,1)} %convert_element_type.9), calls=%async_computation | async-start | bytes 25165824 | tf_op jit(solution)/shard_map/all_to_all | solution.py:10
  34.5 265.0 %copy-start = (f32[256,32]{0,1:T(8,128)S(1)}, f32[256,32]{0,1:T(8,128)}, u32[]{:S(2)}) copy-start(f32[256,32]{0,1:T(8,128)} %param.6) | copy-start | bytes 98308
  34.5 265.0 %copy-start.1 = (f32[256]{0:T(256)S(1)}, f32[256]{0:T(256)}, u32[]{:S(2)}) copy-start(f32[256]{0:T(256)} %param.7) | copy-start | bytes 3076
  294.2 342.1 %all-to-all-start.1 = ((bf16[32,256,768]{2,1,0:T(8,128)(2,1)}), bf16[32,256,768]{2,1,0:T(8,128)(2,1)}, u32[]{:S(2)}, u32[]{:S(2)}) async-start(bf16[32,256,768]{2,1,0:T(8,128)(2,1)} %convert_element_type.10), calls=%async_computation.1 | async-start | bytes 25165824 | tf_op jit(solution)/shard_map/all_to_all | solution.py:11
where the time goes:
time: 675 us; the launch traced here: 673 us
  blocking collectives  299 us (44%)
  waiting for transfers between devices  260 us (39%)
  local copies, waits for them, and re-layouts  73.7 us (11%)
  other arithmetic  26.6 us (4%)
  starting transfers between devices  12.6 us (2%)
    all_gather x1, blocking collectives, on_device(): row_router = lax.all_gather(part_router, 'rows', axis=0, tiled=True)  292 us
    all_to_all x1, waiting for transfers between devices, on_device(): lax.all_to_all(narrow_gate, 'rows', split_axis=0, concat_axis=1, tiled=True)  260 us
    all_to_all x2, local copies, waits for them, and re-layouts, on_device(): lax.all_to_all(narrow_up, 'rows', split_axis=0, concat_axis=1, tiled=True)  36.4 us
    all_to_all x2, local copies, waits for them, and re-layouts, on_device(): lax.all_to_all(narrow_gate, 'rows', split_axis=0, concat_axis=1, tiled=True)  36.3 us
  transfers between devices with their start and end apart: 2, of which 1 were waited for; matrix products, arithmetic and copies ran while one was open for 5% of the time, Pallas kernels for 0%

commit v1 on v0

--- a/solution.py
+++ b/solution.py
@@ -13,7 +13,10 @@
     ready_gate = jnp.transpose(ready_gate, (0, 2, 1))
     ready_up = jnp.transpose(ready_up, (0, 2, 1))
     part_router = (router_weight * router_gain[:, None]).astype(jnp.bfloat16)
-    row_router = lax.all_gather(part_router, "rows", axis=0, tiled=True)
+    size = lax.axis_size("rows")
+    tiles = jnp.stack([part_router for _ in range(size)])
+    tiles = lax.all_to_all(tiles, "rows", split_axis=0, concat_axis=0)
+    row_router = jnp.concatenate(tiles, axis=0)
     serve_router = lax.all_gather(row_router, "owner", axis=1, tiled=True)
     return (ready_gate, ready_up, serve_router)
 

time: 675 us -> 616 us (0.913)
  blocking collectives: 299 us -> 7.2 us
  waiting for transfers between devices: 260 us -> 486 us
    all_gather x1 -> x0, blocking collectives: 292 us -> none  [on_device(): row_router = lax.all_gather(part_router, 'rows', axis=0, tiled=True)]
    all_to_all x1, waiting for transfers between devices: 0.01 us -> 227 us  [on_device(): lax.all_to_all(narrow_up, 'rows', split_axis=0, concat_axis=1, tiled=True)]
    all_to_all x0 -> x1, starting transfers between devices: none -> 7.28 us  [on_device(): tiles = lax.all_to_all(tiles, 'rows', split_axis=0, concat_axis=0)]
  transfers between devices with their start and end apart: 2 -> 3, of which waited for: 1 -> 2; matrix products, arithmetic and copies ran while one was open for 5% -> 7% of each run, Pallas kernels for 0% -> 0%
where the time goes in v1:
time: 616 us; the launch traced here: 614 us
  waiting for transfers between devices  486 us (79%)
  local copies, waits for them, and re-layouts  74.4 us (12%)
  other arithmetic  27.3 us (4%)
  starting transfers between devices  18.6 us (3%)
  blocking collectives  7.2 us (1%)
    all_to_all x1, waiting for transfers between devices, on_device(): lax.all_to_all(narrow_gate, 'rows', split_axis=0, concat_axis=1, tiled=True)  259 us
    all_to_all x1, waiting for transfers between devices, on_device(): lax.all_to_all(narrow_up, 'rows', split_axis=0, concat_axis=1, tiled=True)  227 us
    all_to_all x2, local copies, waits for them, and re-layouts, on_device(): lax.all_to_all(narrow_up, 'rows', split_axis=0, concat_axis=1, tiled=True)  36.4 us
    all_to_all x2, local copies, waits for them, and re-layouts, on_device(): lax.all_to_all(narrow_gate, 'rows', split_axis=0, concat_axis=1, tiled=True)  36.3 us
    convert_element_type x1, other arithmetic, on_device(): train_up.astype(jnp.bfloat16)  13.4 us
    convert_element_type x1, other arithmetic, on_device(): train_gate.astype(jnp.bfloat16)  13.2 us
  transfers between devices with their start and end apart: 3, of which 2 were waited for; matrix products, arithmetic and copies ran while one was open for 7% of the time, Pallas kernels for 0%

profile of v1, /device:TPU:0, one launch (start us, length us, event | category | flops | bytes accessed | tf_op | source)
XLA Modules:
  0.0 614.3 jit_solution(1102473876650567153)
XLA Ops:
  0.6 0.8 multiply_convert_fusion
  1.4 0.7 stack.2
  2.1 7.3 %all-to-all-start.2 = ((bf16[8,256,32]{1,2,0:T(8,128)(2,1)}), bf16[8,256,32]{1,2,0:T(8,128)(2,1)S(1)}, u32[]{:S(2)}, u32[]{:S(2)}) async-start(bf16[8,256,32]{1,2,0:T(8,128)(2,1)} %stack.2), calls=%async_computation.2 | async-start | bytes 262144 | tf_op jit(solution)/shard_map/all_to_all | solution.py:18
  9.3 13.2 %convert_element_type.9 = bf16[32,256,768]{2,1,0:T(8,128)(2,1)} convert(f32[32,256,768]{2,1,0:T(8,128)} %param.4) | non-fusion elementwise | flops 6291456 | bytes 37748736 | tf_op jit(solution)/shard_map/convert_element_type | solution.py:8
  22.5 0.0 all-to-all-done.2
  22.5 6.0 all-to-all-start
  28.5 13.4 %convert_element_type.10 = bf16[32,256,768]{2,1,0:T(8,128)(2,1)} convert(f32[32,256,768]{2,1,0:T(8,128)} %param.5) | non-fusion elementwise | flops 6291456 | bytes 37748736 | tf_op jit(solution)/shard_map/convert_element_type | solution.py:8
  41.9 259.1 %all-to-all-done = bf16[32,256,768]{2,1,0:T(8,128)(2,1)} async-done(((bf16[32,256,768]{2,1,0:T(8,128)(2,1)}), bf16[32,256,768]{2,1,0:T(8,128)(2,1)}, u32[]{:S(2)}, u32[]{:S(2)}) %all-to-all-start) | async-done | bytes 12582944 | tf_op jit(solution)/shard_map/all_to_all | solution.py:10
  301.0 5.3 all-to-all-start.1
  306.4 7.2 %all_gather.3 = bf16[2048,128]{0,1:T(8,128)(2,1)S(1)} all-gather(bf16[2048,32]{0,1:T(8,128)(2,1)S(1)} %bitcast.20), channel_id=1, replica_groups=mesh['owner'=4,'rows'=8] {'owner'}, dimensions={1}, use_global_device_ids=true | all-gather | bytes 655360 | tf_op jit(solution)/shard_map/all_gather | solution.py:20
  313.6 1.0 copy.16
  314.6 16.9 %copy.13 = bf16[8,4,256,768]{2,0,3,1:T(8,128)(2,1)} copy(bf16[8,4,256,768]{3,2,1,0:T(8,128)(2,1)} %bitcast) | data formatting | bytes 25165824 | tf_op jit(solution)/shard_map/all_to_all | solution.py:10
  331.5 19.5 %all_to_all.32 = bf16[4,2048,768]{1,2,0:T(8,128)(2,1)} reshape(bf16[4,8,256,768]{2,1,3,0:T(8,128)(2,1)} %bitcast.16) | data formatting | bytes 25165824 | tf_op jit(solution)/shard_map/all_to_all | solution.py:10
  350.9 227.0 %all-to-all-done.1 = bf16[32,256,768]{2,1,0:T(8,128)(2,1)} async-done(((bf16[32,256,768]{2,1,0:T(8,128)(2,1)}), bf16[32,256,768]{2,1,0:T(8,128)(2,1)}, u32[]{:S(2)}, u32[]{:S(2)}) %all-to-all-start.1) | async-done | bytes 12582944 | tf_op jit(solution)/shard_map/all_to_all | solution.py:11
  578.0 16.9 %copy.14 = bf16[8,4,256,768]{2,0,3,1:T(8,128)(2,1)} copy(bf16[8,4,256,768]{3,2,1,0:T(8,128)(2,1)} %bitcast.3) | data formatting | bytes 25165824 | tf_op jit(solution)/shard_map/all_to_all | solution.py:11
  594.8 19.5 %all_to_all.36 = bf16[4,2048,768]{1,2,0:T(8,128)(2,1)} reshape(bf16[4,8,256,768]{2,1,3,0:T(8,128)(2,1)} %bitcast.17) | data formatting | bytes 25165824 | tf_op jit(solution)/shard_map/all_to_all | solution.py:11
  (1 shorter events, 0.0 us)
Async XLA Ops:
  2.1 20.5 %all-to-all-start.2 = ((bf16[8,256,32]{1,2,0:T(8,128)(2,1)}), bf16[8,256,32]{1,2,0:T(8,128)(2,1)S(1)}, u32[]{:S(2)}, u32[]{:S(2)}) async-start(bf16[8,256,32]{1,2,0:T(8,128)(2,1)} %stack.2), calls=%async_computation.2 | async-start | bytes 262144 | tf_op jit(solution)/shard_map/all_to_all | solution.py:18
  22.5 278.5 %all-to-all-start = ((bf16[32,256,768]{2,1,0:T(8,128)(2,1)}), bf16[32,256,768]{2,1,0:T(8,128)(2,1)}, u32[]{:S(2)}, u32[]{:S(2)}) async-start(bf16[32,256,768]{2,1,0:T(8,128)(2,1)} %convert_element_type.9), calls=%async_computation | async-start | bytes 25165824 | tf_op jit(solution)/shard_map/all_to_all | solution.py:10
  301.0 276.9 %all-to-all-start.1 = ((bf16[32,256,768]{2,1,0:T(8,128)(2,1)}), bf16[32,256,768]{2,1,0:T(8,128)(2,1)}, u32[]{:S(2)}, u32[]{:S(2)}) async-start(bf16[32,256,768]{2,1,0:T(8,128)(2,1)} %convert_element_type.10), calls=%async_computation.1 | async-start | bytes 25165824 | tf_op jit(solution)/shard_map/all_to_all | solution.py:11

commit v2 on v0

--- a/solution.py
+++ b/solution.py
@@ -14,7 +14,14 @@
     ready_up = jnp.transpose(ready_up, (0, 2, 1))
     part_router = (router_weight * router_gain[:, None]).astype(jnp.bfloat16)
     row_router = lax.all_gather(part_router, "rows", axis=0, tiled=True)
-    serve_router = lax.all_gather(row_router, "owner", axis=1, tiled=True)
+    ways = lax.axis_size("owner")
+    pieces = [row_router]
+    for far in range(1, ways):
+        pieces.append(
+            lax.ppermute(pieces[far - 1], "owner", [(d, (d - 1) % ways) for d in range(ways)])
+        )
+    line = jnp.concatenate(pieces, axis=1)
+    serve_router = jnp.roll(line, lax.axis_index("owner") * row_router.shape[1], axis=1)
     return (ready_gate, ready_up, serve_router)
 
 

time: 675 us -> 680 us (level)
  blocking collectives: 299 us -> 292 us
  waiting for transfers between devices: 260 us -> 267 us
    ppermute x0 -> x3, waiting for transfers between devices: none -> 7.53 us  [on_device(): lax.ppermute(pieces[far - 1], 'owner', [(d, (d - 1) % ways) for d in rang...]
    all_gather x1 -> x0, blocking collectives: 7.19 us -> none  [on_device(): serve_router = lax.all_gather(row_router, 'owner', axis=1, tiled=True)]
  transfers between devices with their start and end apart: 2 -> 5, of which waited for: 1 -> 4; matrix products, arithmetic and copies ran while one was open for 5% -> 5% of each run, Pallas kernels for 0% -> 0%
where the time goes in v2:
time: 680 us; the launch traced here: 677 us
  blocking collectives  292 us (43%)
  waiting for transfers between devices  267 us (39%)
  local copies, waits for them, and re-layouts  73.9 us (11%)
  other arithmetic  26.6 us (4%)
  starting transfers between devices  16.4 us (2%)
    all_gather x1, blocking collectives, on_device(): row_router = lax.all_gather(part_router, 'rows', axis=0, tiled=True)  292 us
    all_to_all x1, waiting for transfers between devices, on_device(): lax.all_to_all(narrow_gate, 'rows', split_axis=0, concat_axis=1, tiled=True)  260 us
    all_to_all x2, local copies, waits for them, and re-layouts, on_device(): lax.all_to_all(narrow_up, 'rows', split_axis=0, concat_axis=1, tiled=True)  36.4 us
    all_to_all x2, local copies, waits for them, and re-layouts, on_device(): lax.all_to_all(narrow_gate, 'rows', split_axis=0, concat_axis=1, tiled=True)  36.3 us
  transfers between devices with their start and end apart: 5, of which 4 were waited for; matrix products, arithmetic and copies ran while one was open for 5% of the time, Pallas kernels for 0%

profile of v2, /device:TPU:0, one launch (start us, length us, event | category | flops | bytes accessed | tf_op | source)
XLA Modules:
  0.0 676.9 jit_solution(4411433780305559663)
XLA Ops:
  0.6 13.2 %convert_element_type.9 = bf16[32,256,768]{2,1,0:T(8,128)(2,1)} convert(f32[32,256,768]{2,1,0:T(8,128)} %param.4) | non-fusion elementwise | flops 6291456 | bytes 37748736 | tf_op jit(solution)/shard_map/convert_element_type | solution.py:8
  13.8 7.3 %all-to-all-start = ((bf16[32,256,768]{2,1,0:T(8,128)(2,1)}), bf16[32,256,768]{2,1,0:T(8,128)(2,1)}, u32[]{:S(2)}, u32[]{:S(2)}) async-start(bf16[32,256,768]{2,1,0:T(8,128)(2,1)} %convert_element_type.9), calls=%async_computation | async-start | bytes 25165824 | tf_op jit(solution)/shard_map/all_to_all | solution.py:10
  21.1 13.4 %convert_element_type.10 = bf16[32,256,768]{2,1,0:T(8,128)(2,1)} convert(f32[32,256,768]{2,1,0:T(8,128)} %param.5) | non-fusion elementwise | flops 6291456 | bytes 37748736 | tf_op jit(solution)/shard_map/convert_element_type | solution.py:8
  34.5 0.0 copy-start
  34.5 0.0 copy-start.1
  34.5 259.6 %all-to-all-done = bf16[32,256,768]{2,1,0:T(8,128)(2,1)} async-done(((bf16[32,256,768]{2,1,0:T(8,128)(2,1)}), bf16[32,256,768]{2,1,0:T(8,128)(2,1)}, u32[]{:S(2)}, u32[]{:S(2)}) %all-to-all-start) | async-done | bytes 12582944 | tf_op jit(solution)/shard_map/all_to_all | solution.py:10
  294.2 5.3 all-to-all-start.1
  299.5 0.0 copy-done
  299.5 0.0 copy-done.1
  299.5 292.2 %all_gather.3 = bf16[2048,32]{0,1:T(8,128)(2,1)S(1)} all-gather(bf16[256,32]{0,1:T(8,128)(2,1)S(1)} %multiply_convert_fusion), channel_id=1, replica_groups=mesh['owner'=4,'rows'=8] {'rows'}, dimensions={0}, use_global_device_ids=true | all-gather | bytes 147456 | tf_op jit(solution)/shard_map/all_gather | solution.py:16
  591.7 0.0 collective-permute-start
  591.8 2.5 collective-permute-done
  594.3 1.9 collective-permute-start.1
  596.2 2.5 collective-permute-done.1
  598.7 1.9 collective-permute-start.2
  600.6 2.5 collective-permute-done.2
  603.2 1.0 copy.12
  604.2 16.9 %copy.10 = bf16[8,4,256,768]{2,0,3,1:T(8,128)(2,1)} copy(bf16[8,4,256,768]{3,2,1,0:T(8,128)(2,1)} %bitcast) | data formatting | bytes 25165824 | tf_op jit(solution)/shard_map/all_to_all | solution.py:10
  621.1 19.5 %all_to_all.29 = bf16[4,2048,768]{1,2,0:T(8,128)(2,1)} reshape(bf16[4,8,256,768]{2,1,3,0:T(8,128)(2,1)} %bitcast.14) | data formatting | bytes 25165824 | tf_op jit(solution)/shard_map/all_to_all | solution.py:10
  640.5 0.0 all-to-all-done.1
  640.6 16.9 %copy.11 = bf16[8,4,256,768]{2,0,3,1:T(8,128)(2,1)} copy(bf16[8,4,256,768]{3,2,1,0:T(8,128)(2,1)} %bitcast.3) | data formatting | bytes 25165824 | tf_op jit(solution)/shard_map/all_to_all | solution.py:11
  657.5 19.5 %all_to_all.33 = bf16[4,2048,768]{1,2,0:T(8,128)(2,1)} reshape(bf16[4,8,256,768]{2,1,3,0:T(8,128)(2,1)} %bitcast.15) | data formatting | bytes 25165824 | tf_op jit(solution)/shard_map/all_to_all | solution.py:11
  (10 shorter events, 0.1 us)
Async XLA Ops:
  13.8 280.3 %all-to-all-start = ((bf16[32,256,768]{2,1,0:T(8,128)(2,1)}), bf16[32,256,768]{2,1,0:T(8,128)(2,1)}, u32[]{:S(2)}, u32[]{:S(2)}) async-start(bf16[32,256,768]{2,1,0:T(8,128)(2,1)} %convert_element_type.9), calls=%async_computation | async-start | bytes 25165824 | tf_op jit(solution)/shard_map/all_to_all | solution.py:10
  34.5 265.0 %copy-start = (f32[256,32]{0,1:T(8,128)S(1)}, f32[256,32]{0,1:T(8,128)}, u32[]{:S(2)}) copy-start(f32[256,32]{0,1:T(8,128)} %param.6) | copy-start | bytes 98308
  34.5 265.0 %copy-start.1 = (f32[256]{0:T(256)S(1)}, f32[256]{0:T(256)}, u32[]{:S(2)}) copy-start(f32[256]{0:T(256)} %param.7) | copy-start | bytes 3076
  294.2 346.4 %all-to-all-start.1 = ((bf16[32,256,768]{2,1,0:T(8,128)(2,1)}), bf16[32,256,768]{2,1,0:T(8,128)(2,1)}, u32[]{:S(2)}, u32[]{:S(2)}) async-start(bf16[32,256,768]{2,1,0:T(8,128)(2,1)} %convert_element_type.10), calls=%async_computation.1 | async-start | bytes 25165824 | tf_op jit(solution)/shard_map/all_to_all | solution.py:11
  591.7 2.5 collective-permute-start
  594.3 4.4 collective-permute-start.1
  598.7 4.4 collective-permute-start.2
